TPU v7x, 128 devices: a whole 4x4x4 slice. The times are simulated.
128 devices in a mesh: gx: 4 (over x_lo, core), gy: 4 (over z), gz: 8 (over x_hi, y).
Axes of the slice: x: 4 (x_hi: 2, x_lo: 2; x = x_hi * 2 + x_lo), y: 4, z: 4, core: 2. Of those that a mesh axis runs over, the one named last changes fastest.
Arguments:
- fields: float32 [11, 500, 32, 1024], P(None, 'gx', 'gy', 'gz'), may hold values from -6 to 6
- var_scale: float32 [11], replicated, may hold values from 0.3 to 3
- start_basis: float32 [500, 64], replicated, may hold values from -6 to 6
Outputs:
- factor: float32 [500, 64], replicated
- core: float32 [64, 11, 32, 1024], P('gx', None, 'gy', 'gz')
All inputs are finite; a program needn't handle non-finite values.
Results may differ from a plain program's by a relative error of at most 0.0002.
Values sent between devices are 32-bit elements; how exact they have to be, the bound alone decides.
A program may use at most 128 MiB of HBM per device.

v0:
```python
import jax
import jax.numpy as jnp
from jax import lax
from jax.sharding import PartitionSpec as P

ITERS = 3


def orthonormal(block):
    small = jnp.dot(block.T, block, precision=lax.Precision.HIGHEST)
    lower = jnp.linalg.cholesky(small)
    return jax.scipy.linalg.solve_triangular(lower, block.T, lower=True).T


def per_device(fields, var_scale, start_basis):
    scaled = fields * var_scale[:, None, None, None]
    contract = (((0, 2, 3), (0, 2, 3)), ((), ()))
    swapped = lax.all_to_all(scaled, "gx", split_axis=2, concat_axis=1, tiled=True)
    partial_gram = lax.dot_general(swapped, swapped, contract, precision=lax.Precision.HIGHEST)
    gram = lax.psum(partial_gram, ("gx", "gy", "gz"))
    basis = start_basis
    for step in range(ITERS):
        basis = orthonormal(jnp.dot(gram, basis, precision=lax.Precision.HIGHEST))
    along_rows = (((0,), (1,)), ((), ()))
    full_core = lax.dot_general(basis, swapped, along_rows, precision=lax.Precision.HIGHEST)
    core = lax.all_to_all(full_core, "gx", split_axis=0, concat_axis=2, tiled=True)
    return (basis, core)


def solution(mesh):
    in_specs = (P(None, "gx", "gy", "gz"), P(), P())
    out_specs = (P(), P("gx", None, "gy", "gz"))
    return jax.shard_map(
        per_device, mesh=mesh, in_specs=in_specs, out_specs=out_specs, check_vma=False
    )
```

profile of v0, /device:TPU:1, one launch (start us, length us, event | category | flops | bytes accessed | tf_op | source)
XLA Modules:
  0.0 325.3 jit_solution(2125841500169065226)
XLA Ops:
  7.2 3.1 broadcast_multiply_fusion
  10.3 1.1 copy.22
  11.4 68.0 %all_to_all.36 = f32[11,125,8,128]{3,1,0,2:T(8,128)S(1)} all-to-all(f32[11,125,8,128]{3,1,0,2:T(8,128)S(1)} %copy.22), channel_id=1, replica_groups=mesh['gx'=4,'gy'=4,'gz'=8] {'gx'}, dimensions={2} | all-to-all | bytes 11264000 | tf_op jit(solution)/shard_map/all_to_all | solution.py:18
  79.4 2.9 copy.32
  82.3 6.2 %all_to_all.29 = f32[11,500,2,128]{3,1,2,0:T(8,128)} reshape(f32[11,4,125,2,128]{4,2,1,3,0:T(8,128)} %bitcast.72) | data formatting | bytes 11264000 | tf_op jit(solution)/shard_map/all_to_all | solution.py:18
  88.5 13.6 %convolution_bitcast_fusion = f32[500,500]{1,0:T(8,128)} fusion(f32[11,500,2,128]{3,1,2,0:T(8,128)} %all_to_all.29), kind=kOutput, calls=%fused_computation.2 | convolution fusion | flops 8448000000 | bytes 6632000 | tf_op jit(solution)/shard_map/dot_general | solution.py:19
  102.1 151.0 %all-reduce.2.cloned.1.call-done = f32[500,500]{1,0:T(8,128)} async-done(((f32[500,500]{1,0:T(8,128)}), f32[500,500]{1,0:T(8,128)}) %all-reduce.2.cloned.1.call-update) | async-done | bytes 1000016 | tf_op jit(solution)/shard_map/psum | solution.py:20
  253.1 2.3 fusion.21
  255.4 0.3 fusion.22
  255.7 5.8 %cholesky.59 = f32[64,64]{1,0:T(8,128)S(1)} custom-call(f32[64,64]{1,0:T(8,128)S(1)} %fusion.16), custom_call_target="Cholesky" | custom-call | tf_op jit(solution)/shard_map/jit(cholesky)/cholesky | solution.py:11
  261.6 0.6 compare_reduce_fusion.2
  262.3 0.7 fusion.8
  262.9 4.9 %custom-call.7 = f32[1,64,64]{1,2,0:T(8,128)S(1)} custom-call(f32[1,64,64]{2,1,0:T(8,128)S(1)} %fusion.8), custom_call_target="InvertDiagBlocksLowerTriangular" | custom-call | tf_op jit(solution)/shard_map/jit(_solve_triangular)/triangular_solve | solution.py:12
  267.8 0.3 fusion.6
  268.2 2.3 fusion.23
  270.5 0.3 fusion.24
  270.8 5.8 %cholesky.70 = f32[64,64]{1,0:T(8,128)S(1)} custom-call(f32[64,64]{1,0:T(8,128)S(1)} %fusion.14), custom_call_target="Cholesky" | custom-call | tf_op jit(solution)/shard_map/jit(cholesky)/cholesky | solution.py:11
  276.7 0.6 compare_reduce_fusion.1
  277.3 0.7 fusion.9
  278.0 4.9 %custom-call.8 = f32[1,64,64]{1,2,0:T(8,128)S(1)} custom-call(f32[1,64,64]{2,1,0:T(8,128)S(1)} %fusion.9), custom_call_target="InvertDiagBlocksLowerTriangular" | custom-call | tf_op jit(solution)/shard_map/jit(_solve_triangular)/triangular_solve | solution.py:12
  282.9 0.3 fusion.4
  283.2 2.3 fusion.25
  285.5 0.3 fusion.26
  285.9 5.8 %cholesky.81 = f32[64,64]{1,0:T(8,128)S(1)} custom-call(f32[64,64]{1,0:T(8,128)S(1)} %fusion.12), custom_call_target="Cholesky" | custom-call | tf_op jit(solution)/shard_map/jit(cholesky)/cholesky | solution.py:11
  291.8 0.6 compare_reduce_fusion
  292.4 0.7 fusion.10
  293.1 4.9 %custom-call.9 = f32[1,64,64]{1,2,0:T(8,128)S(1)} custom-call(f32[1,64,64]{2,1,0:T(8,128)S(1)} %fusion.10), custom_call_target="InvertDiagBlocksLowerTriangular" | custom-call | tf_op jit(solution)/shard_map/jit(_solve_triangular)/triangular_solve | solution.py:12
  298.0 0.3 fusion.2
  298.3 6.1 %fusion = f32[64,11,2,128]{3,0,2,1:T(8,128)S(1)} fusion(f32[11,500,2,128]{3,1,2,0:T(8,128)} %all_to_all.29, f32[64,500]{1,0:T(8,128)S(1)} %fusion.2), kind=kOutput, calls=%fused_computation.3 | convolution fusion | flops 1081344000 | bytes 6480896 | tf_op jit(solution)/shard_map/dot_general | solution.py:25
  304.5 0.6 copy.27
  305.0 12.3 %all_to_all.37 = f32[64,11,2,128]{3,2,1,0:T(2,128)S(1)} all-to-all(f32[64,11,2,128]{3,2,1,0:T(2,128)S(1)} %copy.27), channel_id=1, replica_groups=mesh['gx'=4,'gy'=4,'gz'=8] {'gx'}, dimensions={0} | all-to-all | bytes 1441792 | tf_op jit(solution)/shard_map/all_to_all | solution.py:26
  317.3 1.1 copy.28
  (15 shorter events, 0.4 us)
Async XLA Ops:
  7.2 245.9 %copy-start = (f32[500,64]{0,1:T(8,128)S(1)}, f32[500,64]{0,1:T(8,128)}, u32[]{:S(2)}) copy-start(f32[500,64]{0,1:T(8,128)} %param.8) | copy-start | bytes 384004
  7.2 245.9 %all-reduce.2.cloned.1.call-start = ((), (), s32[]{:S(2)}) async-start(), calls=%async_computation.2 | async-start | bytes 2064384 | tf_op jit(solution)/shard_map/psum | solution.py:20
  298.3 20.1 %copy-start.1 = (f32[64,500]{1,0:T(8,128)}, f32[64,500]{1,0:T(8,128)S(1)}, u32[]{:S(2)}) copy-start(f32[64,500]{1,0:T(8,128)S(1)} %fusion.2) | copy-start | bytes 384004
Sparse Core Ops, SparseCore 0:
  102.3 150.8 all-reduce.1
where the time goes:
time: 326 us; the launch traced here: 325 us
  waiting for transfers between devices  151 us (46%)
  blocking collectives  80.3 us (25%)
  other arithmetic  39.3 us (12%)
  matrix products  28.4 us (9%)
  between operations  14.2 us (4%)
  local copies, waits for them, and re-layouts  12.1 us (4%)
    psum x1, waiting for transfers between devices, per_device(): gram = lax.psum(partial_gram, ('gx', 'gy', 'gz'))  151 us
    all_to_all x1, blocking collectives, per_device(): lax.all_to_all(scaled, 'gx', split_axis=2, concat_axis=1, tiled=True)  68 us
    another operation x9, other arithmetic, orthonormal(): lower = jnp.linalg.cholesky(small)  19.6 us
    another operation x6, other arithmetic, orthonormal(): return jax.scipy.linalg.solve_triangular(lower, block.T, lower=True).T  16.6 us
    dot_general x1, matrix products, per_device(): lax.dot_general(swapped, swapped, contract, precision=lax.Precision.HIGHEST)  13.6 us
    all_to_all x1, blocking collectives, per_device(): lax.all_to_all(full_core, 'gx', split_axis=0, concat_axis=2, tiled=True)  12.3 us
    all_to_all x2, local copies, waits for them, and re-layouts, per_device(): lax.all_to_all(scaled, 'gx', split_axis=2, concat_axis=1, tiled=True)  9.05 us
    dot_general x3, matrix products, per_device(): basis = orthonormal(jnp.dot(gram, basis, precision=lax.Precision.HIGHEST))  6.83 us
  transfers between devices with their start and end apart: 1, of which 1 were waited for; matrix products, arithmetic and copies ran while one was open for 0% of the time, Pallas kernels for 0%

commit v1 on v0

--- a/solution.py
+++ b/solution.py
@@ -17,7 +17,7 @@
     contract = (((0, 2, 3), (0, 2, 3)), ((), ()))
     swapped = lax.all_to_all(scaled, "gx", split_axis=2, concat_axis=1, tiled=True)
     partial_gram = lax.dot_general(swapped, swapped, contract, precision=lax.Precision.HIGHEST)
-    gram = lax.psum(partial_gram, ("gx", "gy", "gz"))
+    gram = lax.psum(lax.psum(partial_gram, ("gy", "gz")), "gx")
     basis = start_basis
     for step in range(ITERS):
         basis = orthonormal(jnp.dot(gram, basis, precision=lax.Precision.HIGHEST))

time: 326 us -> 577 us (1.77)
  waiting for transfers between devices: 151 us -> 401 us
    psum x1 -> x2, waiting for transfers between devices: 151 us -> 401 us  [per_device(): gram = lax.psum(lax.psum(partial_gram, ('gy', 'gz')), 'gx')]
  transfers between devices with their start and end apart: 1 -> 2, of which waited for: 1 -> 2; matrix products, arithmetic and copies ran while one was open for 0% -> 0% of each run, Pallas kernels for 0% -> 0%
where the time goes in v1:
time: 577 us; the launch traced here: 576 us
  waiting for transfers between devices  401 us (69%)
  blocking collectives  81 us (14%)
  other arithmetic  39.3 us (7%)
  matrix products  28.4 us (5%)
  between operations  14.2 us (2%)
  local copies, waits for them, and re-layouts  12.1 us (2%)
    psum x2, waiting for transfers between devices, per_device(): gram = lax.psum(lax.psum(partial_gram, ('gy', 'gz')), 'gx')  401 us
    all_to_all x1, blocking collectives, per_device(): lax.all_to_all(scaled, 'gx', split_axis=2, concat_axis=1, tiled=True)  68 us
    another operation x9, other arithmetic, orthonormal(): lower = jnp.linalg.cholesky(small)  19.6 us
    another operation x6, other arithmetic, orthonormal(): return jax.scipy.linalg.solve_triangular(lower, block.T, lower=True).T  16.6 us
    dot_general x1, matrix products, per_device(): lax.dot_general(swapped, swapped, contract, precision=lax.Precision.HIGHEST)  13.6 us
    all_to_all x1, blocking collectives, per_device(): lax.all_to_all(full_core, 'gx', split_axis=0, concat_axis=2, tiled=True)  13 us
  transfers between devices with their start and end apart: 2, of which 2 were waited for; matrix products, arithmetic and copies ran while one was open for 0% of the time, Pallas kernels for 0%

profile of v1, /device:TPU:1, one launch (start us, length us, event | category | flops | bytes accessed | tf_op | source)
XLA Modules:
  0.0 576.1 jit_solution(7991892348294177944)
XLA Ops:
  7.2 3.1 broadcast_multiply_fusion
  10.3 1.1 copy.22
  11.4 68.0 %all_to_all.36 = f32[11,125,8,128]{3,1,0,2:T(8,128)S(1)} all-to-all(f32[11,125,8,128]{3,1,0,2:T(8,128)S(1)} %copy.22), channel_id=1, replica_groups=mesh['gx'=4,'gy'=4,'gz'=8] {'gx'}, dimensions={2} | all-to-all | bytes 11264000 | tf_op jit(solution)/shard_map/all_to_all | solution.py:18
  79.4 2.9 copy.32
  82.3 6.2 %all_to_all.29 = f32[11,500,2,128]{3,1,2,0:T(8,128)} reshape(f32[11,4,125,2,128]{4,2,1,3,0:T(8,128)} %bitcast.72) | data formatting | bytes 11264000 | tf_op jit(solution)/shard_map/all_to_all | solution.py:18
  88.5 13.6 %convolution_bitcast_fusion = f32[500,500]{1,0:T(8,128)} fusion(f32[11,500,2,128]{3,1,2,0:T(8,128)} %all_to_all.29), kind=kOutput, calls=%fused_computation.2 | convolution fusion | flops 8448000000 | bytes 6632000 | tf_op jit(solution)/shard_map/dot_general | solution.py:19
  102.4 334.6 %all-reduce.3.cloned.1.call-done = f32[500,500]{1,0:T(8,128)} async-done(((f32[500,500]{1,0:T(8,128)}), f32[500,500]{1,0:T(8,128)}) %all-reduce.3.cloned.1.call-update) | async-done | bytes 1000016 | tf_op jit(solution)/shard_map/psum | solution.py:20
  437.0 66.3 %all-reduce.5.cloned.1.call-done = f32[500,500]{1,0:T(8,128)} async-done(((f32[500,500]{1,0:T(8,128)}), f32[500,500]{1,0:T(8,128)}) %all-reduce.5.cloned.1.call-update) | async-done | bytes 1000016 | tf_op jit(solution)/shard_map/psum | solution.py:20
  503.3 2.3 fusion.21
  506.0 5.8 %cholesky.59 = f32[64,64]{1,0:T(8,128)S(1)} custom-call(f32[64,64]{1,0:T(8,128)S(1)} %fusion.16), custom_call_target="Cholesky" | custom-call | tf_op jit(solution)/shard_map/jit(cholesky)/cholesky | solution.py:11
  511.9 0.6 compare_reduce_fusion.2
  512.5 0.7 fusion.8
  513.2 4.9 custom-call.7
  518.1 0.3 fusion.6
  518.4 2.3 fusion.23
  520.7 0.3 fusion.24
  521.0 5.8 %cholesky.70 = f32[64,64]{1,0:T(8,128)S(1)} custom-call(f32[64,64]{1,0:T(8,128)S(1)} %fusion.14), custom_call_target="Cholesky" | custom-call | tf_op jit(solution)/shard_map/jit(cholesky)/cholesky | solution.py:11
  526.9 0.6 compare_reduce_fusion.1
  527.6 0.7 fusion.9
  528.2 4.9 custom-call.8
  533.1 0.3 fusion.4
  533.5 2.3 fusion.25
  535.8 0.3 fusion.26
  536.1 5.8 %cholesky.81 = f32[64,64]{1,0:T(8,128)S(1)} custom-call(f32[64,64]{1,0:T(8,128)S(1)} %fusion.12), custom_call_target="Cholesky" | custom-call | tf_op jit(solution)/shard_map/jit(cholesky)/cholesky | solution.py:11
  542.0 0.6 compare_reduce_fusion
  542.6 0.7 fusion.10
  543.3 4.9 custom-call.9
  548.2 0.3 fusion.2
  548.6 6.1 %fusion = f32[64,11,2,128]{3,0,2,1:T(8,128)S(1)} fusion(f32[11,500,2,128]{3,1,2,0:T(8,128)} %all_to_all.29, f32[64,500]{1,0:T(8,128)S(1)} %fusion.2), kind=kOutput, calls=%fused_computation.3 | convolution fusion | flops 1081344000 | bytes 6480896 | tf_op jit(solution)/shard_map/dot_general | solution.py:25
  554.7 0.6 copy.27
  555.2 13.0 %all_to_all.37 = f32[64,11,2,128]{3,2,1,0:T(2,128)S(1)} all-to-all(f32[64,11,2,128]{3,2,1,0:T(2,128)S(1)} %copy.27), channel_id=1, replica_groups=mesh['gx'=4,'gy'=4,'gz'=8] {'gx'}, dimensions={0} | all-to-all | bytes 1441792 | tf_op jit(solution)/shard_map/all_to_all | solution.py:26
  568.2 1.1 copy.28
  (18 shorter events, 0.9 us)
Async XLA Ops:
  7.2 496.2 %copy-start = (f32[500,64]{0,1:T(8,128)S(1)}, f32[500,64]{0,1:T(8,128)}, u32[]{:S(2)}) copy-start(f32[500,64]{0,1:T(8,128)} %param.8) | copy-start | bytes 384004
  7.2 429.8 %all-reduce.3.cloned.1.call-start = ((), (), s32[]{:S(2)}) async-start(), calls=%async_computation.2 | async-start | bytes 2064384 | tf_op jit(solution)/shard_map/psum | solution.py:20
  102.1 401.2 %all-reduce.5.cloned.1.call-start = ((), (), s32[]{:S(2)}) async-start(), calls=%async_computation.3 | async-start | bytes 2064384 | tf_op jit(solution)/shard_map/psum | solution.py:20
  548.5 20.8 %copy-start.1 = (f32[64,500]{1,0:T(8,128)}, f32[64,500]{1,0:T(8,128)S(1)}, u32[]{:S(2)}) copy-start(f32[64,500]{1,0:T(8,128)S(1)} %fusion.2) | copy-start | bytes 384004
Sparse Core Ops, SparseCore 0:
  102.3 334.6 all-reduce.2
  439.5 63.7 all-reduce.4

commit v2 on v0

--- a/solution.py
+++ b/solution.py
@@ -15,7 +15,10 @@
 def per_device(fields, var_scale, start_basis):
     scaled = fields * var_scale[:, None, None, None]
     contract = (((0, 2, 3), (0, 2, 3)), ((), ()))
-    swapped = lax.all_to_all(scaled, "gx", split_axis=2, concat_axis=1, tiled=True)
+    swapped = jnp.concatenate(
+        lax.all_to_all(jnp.stack(jnp.split(scaled, lax.axis_size("gx"), axis=2)), "gx", 0, 0),
+        axis=1,
+    )
     partial_gram = lax.dot_general(swapped, swapped, contract, precision=lax.Precision.HIGHEST)
     gram = lax.psum(partial_gram, ("gx", "gy", "gz"))
     basis = start_basis

time: 326 us -> 329 us (level)
    reshape x0 -> x2, local copies, waits for them, and re-layouts: none -> 9.44 us  [per_device(): jnp.concatenate(lax.all_to_all(jnp.stack(jnp.split(scaled, lax.axis_size(...]
    all_to_all x2 -> x0, local copies, waits for them, and re-layouts: 9.05 us -> none  [per_device(): lax.all_to_all(scaled, 'gx', split_axis=2, concat_axis=1, tiled=True)]
where the time goes in v2:
time: 329 us; the launch traced here: 328 us
  waiting for transfers between devices  151 us (46%)
  blocking collectives  78.8 us (24%)
  other arithmetic  42.3 us (13%)
  matrix products  28.4 us (9%)
  between operations  14.2 us (4%)
  local copies, waits for them, and re-layouts  13.4 us (4%)
    psum x1, waiting for transfers between devices, per_device(): gram = lax.psum(partial_gram, ('gx', 'gy', 'gz'))  151 us
    all_to_all x1, blocking collectives, per_device(): lax.all_to_all(jnp.stack(jnp.split(scaled, lax.axis_size('gx'), axis=2)),...  66.6 us
    another operation x9, other arithmetic, orthonormal(): lower = jnp.linalg.cholesky(small)  19.6 us
    another operation x6, other arithmetic, orthonormal(): return jax.scipy.linalg.solve_triangular(lower, block.T, lower=True).T  16.6 us
    dot_general x1, matrix products, per_device(): lax.dot_general(swapped, swapped, contract, precision=lax.Precision.HIGHEST)  13.6 us
    all_to_all x1, blocking collectives, per_device(): lax.all_to_all(full_core, 'gx', split_axis=0, concat_axis=2, tiled=True)  12.3 us
    reshape x2, local copies, waits for them, and re-layouts, per_device(): jnp.concatenate(lax.all_to_all(jnp.stack(jnp.split(scaled, lax.axis_size(...  9.44 us
    dot_general x3, matrix products, per_device(): basis = orthonormal(jnp.dot(gram, basis, precision=lax.Precision.HIGHEST))  6.83 us
  transfers between devices with their start and end apart: 1, of which 1 were waited for; matrix products, arithmetic and copies ran while one was open for 0% of the time, Pallas kernels for 0%

profile of v2, /device:TPU:1, one launch (start us, length us, event | category | flops | bytes accessed | tf_op | source)
XLA Modules:
  0.0 328.1 jit_solution(1241575874143370499)
XLA Ops:
  7.2 3.1 broadcast_multiply_fusion
  10.3 2.0 slice_bitcast_fusion.3
  12.3 3.0 pad_maximum_fusion
  15.3 66.6 %all_to_all.23 = f32[4,11,125,2,128]{4,3,2,1,0:T(2,128)S(1)} all-to-all(f32[4,11,125,2,128]{4,3,2,1,0:T(2,128)S(1)} %pad_maximum_fusion), channel_id=1, replica_groups=mesh['gx'=4,'gy'=4,'gz'=8] {'gx'}, dimensions={0} | all-to-all | bytes 11264000 | tf_op jit(solution)/shard_map/all_to_all | solution.py:19
  81.9 3.3 copy.15
  85.1 6.2 %reshape.20 = f32[11,500,2,128]{3,1,2,0:T(8,128)} reshape(f32[11,4,125,2,128]{4,2,1,3,0:T(8,128)} %copy.15) | data formatting | bytes 11264000 | tf_op jit(solution)/shard_map/reshape | solution.py:18
  91.3 13.6 %convolution_bitcast_fusion = f32[500,500]{1,0:T(8,128)} fusion(f32[11,500,2,128]{3,1,2,0:T(8,128)} %reshape.20), kind=kOutput, calls=%fused_computation.6 | convolution fusion | flops 8448000000 | bytes 6632000 | tf_op jit(solution)/shard_map/dot_general | solution.py:22
  105.0 150.9 %all-reduce.2.cloned.1.call-done = f32[500,500]{1,0:T(8,128)} async-done(((f32[500,500]{1,0:T(8,128)}), f32[500,500]{1,0:T(8,128)}) %all-reduce.2.cloned.1.call-update) | async-done | bytes 1000016 | tf_op jit(solution)/shard_map/psum | solution.py:23
  255.9 2.3 fusion.21
  258.2 0.3 fusion.22
  258.6 5.8 %cholesky.59 = f32[64,64]{1,0:T(8,128)S(1)} custom-call(f32[64,64]{1,0:T(8,128)S(1)} %fusion.16), custom_call_target="Cholesky" | custom-call | tf_op jit(solution)/shard_map/jit(cholesky)/cholesky | solution.py:11
  264.4 0.6 compare_reduce_fusion.2
  265.1 0.7 fusion.8
  265.7 4.9 %custom-call.7 = f32[1,64,64]{1,2,0:T(8,128)S(1)} custom-call(f32[1,64,64]{2,1,0:T(8,128)S(1)} %fusion.8), custom_call_target="InvertDiagBlocksLowerTriangular" | custom-call | tf_op jit(solution)/shard_map/jit(_solve_triangular)/triangular_solve | solution.py:12
  270.6 0.3 fusion.6
  271.0 2.3 fusion.23
  273.6 5.8 %cholesky.70 = f32[64,64]{1,0:T(8,128)S(1)} custom-call(f32[64,64]{1,0:T(8,128)S(1)} %fusion.14), custom_call_target="Cholesky" | custom-call | tf_op jit(solution)/shard_map/jit(cholesky)/cholesky | solution.py:11
  279.5 0.6 compare_reduce_fusion.1
  280.2 0.7 fusion.9
  280.8 4.9 %custom-call.8 = f32[1,64,64]{1,2,0:T(8,128)S(1)} custom-call(f32[1,64,64]{2,1,0:T(8,128)S(1)} %fusion.9), custom_call_target="InvertDiagBlocksLowerTriangular" | custom-call | tf_op jit(solution)/shard_map/jit(_solve_triangular)/triangular_solve | solution.py:12
  285.7 0.3 fusion.4
  286.1 2.3 fusion.25
  288.3 0.3 fusion.26
  288.7 5.8 %cholesky.81 = f32[64,64]{1,0:T(8,128)S(1)} custom-call(f32[64,64]{1,0:T(8,128)S(1)} %fusion.12), custom_call_target="Cholesky" | custom-call | tf_op jit(solution)/shard_map/jit(cholesky)/cholesky | solution.py:11
  294.6 0.6 compare_reduce_fusion
  295.2 0.7 fusion.10
  295.9 4.9 %custom-call.9 = f32[1,64,64]{1,2,0:T(8,128)S(1)} custom-call(f32[1,64,64]{2,1,0:T(8,128)S(1)} %fusion.10), custom_call_target="InvertDiagBlocksLowerTriangular" | custom-call | tf_op jit(solution)/shard_map/jit(_solve_triangular)/triangular_solve | solution.py:12
  300.8 0.3 fusion.2
  301.1 6.1 %fusion = f32[64,11,2,128]{3,0,2,1:T(8,128)S(1)} fusion(f32[11,500,2,128]{3,1,2,0:T(8,128)} %reshape.20, f32[64,500]{1,0:T(8,128)S(1)} %fusion.2), kind=kOutput, calls=%fused_computation.7 | convolution fusion | flops 1081344000 | bytes 6480896 | tf_op jit(solution)/shard_map/dot_general | solution.py:28
  307.3 0.6 copy.19
  307.8 12.3 %all_to_all.24 = f32[64,11,2,128]{3,2,1,0:T(2,128)S(1)} all-to-all(f32[64,11,2,128]{3,2,1,0:T(2,128)S(1)} %copy.19), channel_id=1, replica_groups=mesh['gx'=4,'gy'=4,'gz'=8] {'gx'}, dimensions={0} | all-to-all | bytes 1441792 | tf_op jit(solution)/shard_map/all_to_all | solution.py:29
  320.1 1.1 copy.20
  (16 shorter events, 0.7 us)
Async XLA Ops:
  7.2 248.8 %copy-start = (f32[500,64]{0,1:T(8,128)S(1)}, f32[500,64]{0,1:T(8,128)}, u32[]{:S(2)}) copy-start(f32[500,64]{0,1:T(8,128)} %param.8) | copy-start | bytes 384004
  7.2 248.7 %all-reduce.2.cloned.1.call-start = ((), (), s32[]{:S(2)}) async-start(), calls=%async_computation.2 | async-start | bytes 2064384 | tf_op jit(solution)/shard_map/psum | solution.py:23
  301.1 20.1 %copy-start.1 = (f32[64,500]{1,0:T(8,128)}, f32[64,500]{1,0:T(8,128)S(1)}, u32[]{:S(2)}) copy-start(f32[64,500]{1,0:T(8,128)S(1)} %fusion.2) | copy-start | bytes 384004
Sparse Core Ops, SparseCore 0:
  105.1 150.7 all-reduce.1
